TPU v7x, 32 devices: a whole 2x2x4 slice. The times are simulated.
32 devices in a mesh: layer: 8 (over z, x), split: 4 (over y, core).
Axes of the slice: x: 2, y: 2, z: 4, core: 2. Of those that a mesh axis runs over, the one named last changes fastest.
Arguments:
- right_side: float32 [32, 512, 128], P('layer', 'split'), may hold values from -6 to 6
- diagonal: float32 [32, 512, 128], P('layer', 'split'), may hold values from 0.1 to 1
- inverses: float32 [32, 512, 512], P('layer', None, 'split'), may hold values from -1 to 1, as said below
Outputs:
- solution_field: float32 [32, 512, 128], P('layer', 'split')
- residual: float32 [32, 512, 128], P('layer', 'split')
Inputs may be any that keep to these rules, and one draw needn't show every extreme that they name: `inverses`: each plane's inverse is a diagonal matrix with entries between 0.5 and 1 plus a dense coupling with zero diagonal and spectral norm below 0.2.
All inputs are finite; a program needn't handle non-finite values.
Results may differ from a plain program's by a relative error of at most 0.0003.
Values sent between devices are 32-bit elements; how exact they have to be, the bound alone decides.
No kernel may reach another device: no remote copies, remote signals or barrier semaphores. Data moves between devices by JAX's collectives and lax.ppermute only.
A program may use at most 64 MiB of HBM per device.

v0:
```python
import jax
import jax.numpy as jnp
from jax import lax
from jax.sharding import PartitionSpec as P


def with_halo(x, sides, width):
    for axis, dim in sides:
        size, length = (lax.axis_size(axis), x.shape[dim])
        up = [(i, (i + 1) % size) for i in range(size - 1)]
        down = [(j, i) for i, j in up]
        last = lax.slice_in_dim(x, length - width, length, axis=dim)
        first = lax.slice_in_dim(x, 0, width, axis=dim)
        before = lax.ppermute(last, axis, up)
        after = lax.ppermute(first, axis, down)
        x = jnp.concatenate([before, x, after], axis=dim)
    return x


def from_behind(block, axis, distance):
    devices = range(lax.axis_size(axis))
    route = [(i - distance, i) for i in devices if i - distance in devices]
    return lax.ppermute(block, axis, route)


def stencil(values, diagonal):
    padded = with_halo(values, (("layer", 0), ("split", 1)), 1)
    beside = padded[2:, 1:-1, :] + padded[:-2, 1:-1, :]
    beside = beside + padded[1:-1, 2:, :] + padded[1:-1, :-2, :]
    centre_part = padded[1:-1, 1:-1, :]
    y_upper = jnp.pad(centre_part[:, :, 1:], ((0, 0), (0, 0), (0, 1)))
    y_lower = jnp.pad(centre_part[:, :, :-1], ((0, 0), (0, 0), (1, 0)))
    return (6.0 + diagonal) * values - beside - y_upper - y_lower


def down_local(matrices, portion, carried):

    def down_advance(state, inputs):
        matrix, source = inputs
        state = jnp.dot(matrix, source + state, precision=lax.Precision.HIGHEST)
        return (state, state)

    return lax.scan(down_advance, carried, (matrices, portion))


def up_local(matrices, portion, carried):

    def up_advance(state, inputs):
        matrix, below = inputs
        state = below + jnp.dot(matrix, state, precision=lax.Precision.HIGHEST)
        return (state, state)

    return lax.scan(up_advance, carried, (matrices, portion), reverse=True)


def chain_sweep(sweep_fn, matrices, source, sender, anchor, nblocks):
    depth_count = lax.axis_size("layer")
    block_width = source.shape[2] // nblocks
    plane_shape = (source.shape[1], block_width)
    result = jnp.zeros_like(source)
    incoming = jnp.zeros(plane_shape, jnp.float32)

    def chain_advance(turn, state):
        result, incoming = state
        block_raw = turn - anchor
        active = jnp.logical_and(block_raw >= 0, block_raw < nblocks)

        def working(unused):
            return sweep_fn(matrices, source, incoming)

        def resting(unused):
            return (jnp.zeros(plane_shape, jnp.float32), jnp.zeros_like(source))

        outgoing, stacked = lax.cond(active, working, resting, None)
        previous = result
        result = jnp.where(active, stacked, previous)
        return (result, sender(outgoing))

    result, incoming = lax.fori_loop(
        0, depth_count + nblocks - 1, chain_advance, (result, incoming)
    )
    return result


def per_device(right_side, diagonal, inverses):
    matrices = lax.all_gather(inverses, "split", axis=2, tiled=True)
    columns = lax.all_to_all(right_side, "split", split_axis=2, concat_axis=1, tiled=True)
    nblocks = 1
    own_index = lax.axis_index("layer")
    depth_count = lax.axis_size("layer")
    applied_rhs = stencil(right_side, diagonal)

    def send_down(values):
        return from_behind(values, "layer", 1)

    def send_up(values):
        return from_behind(values, "layer", -1)

    lower_sweep = chain_sweep(down_local, matrices, columns, send_down, own_index, nblocks)
    upper_sweep = chain_sweep(
        up_local, matrices, lower_sweep, send_up, depth_count - 1 - own_index, nblocks
    )
    direction = lax.all_to_all(upper_sweep, "split", split_axis=1, concat_axis=2, tiled=True)
    image = stencil(direction, diagonal)
    applied_image = stencil(image, diagonal)
    sums_all = lax.psum(
        (
            jnp.sum(right_side * right_side),
            jnp.sum(right_side * image),
            jnp.sum(applied_rhs * right_side),
            jnp.sum(applied_rhs * image),
            jnp.sum(applied_image * right_side),
            jnp.sum(applied_image * image),
            jnp.sum(applied_rhs * applied_rhs),
            jnp.sum(applied_rhs * applied_image),
            jnp.sum(applied_image * applied_image),
        ),
        ("layer", "split"),
    )
    (
        norm_sq,
        curv_sum,
        rhs_rhs,
        rhs_image,
        image_rhs,
        image_image,
        arhs_arhs,
        arhs_aimage,
        aimage_aimage,
    ) = sums_all
    step_alpha = norm_sq / curv_sum
    middle = right_side - step_alpha * image
    tangent = applied_rhs - step_alpha * applied_image
    cross_sum = (
        rhs_rhs - step_alpha * (rhs_image + image_rhs) + step_alpha * step_alpha * image_image
    )
    self_sum = arhs_arhs - 2.0 * step_alpha * arhs_aimage + step_alpha * step_alpha * aimage_aimage
    step_omega = cross_sum / self_sum
    solution_field = step_alpha * direction + step_omega * middle
    residual = middle - step_omega * tangent
    return (solution_field, residual)


def solution(mesh):
    placed = (P("layer", "split", None), P("layer", "split", None), P("layer", None, "split"))
    return jax.shard_map(
        per_device,
        mesh=mesh,
        in_specs=placed,
        out_specs=(P("layer", "split", None), P("layer", "split", None)),
        check_vma=False,
    )
```

profile of v0, /device:TPU:12, one launch (start us, length us, event | category | flops | bytes accessed | tf_op | source)
XLA Modules:
  0.0 438.9 jit_solution(2182941142321325081)
XLA Ops:
  7.9 1.8 copy.44
  9.7 3.9 all-to-all-start
  14.7 3.3 collective-permute-start.6
  18.0 2.6 collective-permute-start.7
  23.4 21.4 %all-gather.2.cloned.1.call-done = f32[4,512,512]{2,1,0:T(8,128)} async-done(((f32[4,512,128]{2,1,0:T(8,128)}), f32[4,512,512]{2,1,0:T(8,128)}) %all-gather.2.cloned.1.call-update) | async-done | bytes 4194320 | tf_op jit(solution)/shard_map/all_gather | solution.py:86
  44.8 112.2 %while.60 = (s32[]{:T(128)}, f32[4,512,32]{1,2,0:T(8,128)S(1)}, f32[512,32]{0,1:T(8,128)S(1)}, s32[]{:T(128)}, f32[4,512,512]{2,1,0:T(8,128)}, /*index=5*/f32[4,512,32]{1,2,0:T(8,128)S(1)}, s32[]{:T(128)}, s32[]{:T(128)}) while((s32[]{:T(128)}, f32[4,512,32]{1,2,0:T(8,128)S(1)}, f32[512,32]{0,1:T(8,128)S(1)}, s32[]{:T(128)}, ...), condition=%wide.region_7.8_spmd.clone, body=%wide.region_2.7_spmd.clone.sunk | while | flops 100810760 | bytes 2623315 | solution.py:79
  45.5 3.4 collective-permute-start.1
  49.0 3.6 collective-permute-done.1
  53.3 2.5 collective-permute-start.1
  55.9 22.0 %collective-permute-done.1 = f32[512,32]{0,1:T(8,128)S(1)} collective-permute-done((f32[512,32]{0,1:T(8,128)S(1)}, f32[512,32]{0,1:T(8,128)S(1)}, u32[]{:S(2)}, u32[]{:S(2)}) %collective-permute-start.1) | collective-permute-done | bytes 65568 | tf_op jit(solution)/shard_map/while/body/eval_jaxpr/ppermute | solution.py:23
  77.9 11.7 %conditional.6 = (f32[512,32]{0,1:T(8,128)S(1)}, f32[4,512,32]{1,2,0:T(8,128)}) conditional(s32[]{:T(128)} %convert_element_type.26, () %tuple.150, (f32[4,512,512]{2,1,0:T(8,128)}, f32[4,512,32]{1,2,0:T(8,128)S(1)}, f32[512,32]{0,1:T(8,128)S(1)}) %tuple.151), branch_computations={%region_3.3_spmd, %region_4.6_spmd} | conditional | flops 100679680 | bytes 1574541 | solution.py:74
  77.9 11.7 %while.58 = (s32[]{:T(128)}, f32[512,32]{0,1:T(8,128)S(1)}, f32[4,512,32]{1,2,0:T(8,128)}, f32[4,512,512]{2,1,0:T(8,128)}, f32[4,512,32]{1,2,0:T(8,128)S(1)}, /*index=5*/s32[]{:T(128)}) while((s32[]{:T(128)}, f32[512,32]{0,1:T(8,128)S(1)}, f32[4,512,32]{1,2,0:T(8,128)}, f32[4,512,512]{2,1,0:T(8,128)}, f32[4,512,32]{1,2,0:T(8,128)S(1)}, ...), condition=%wide.region_6.5_spmd, body=%wide.region_5.4_spmd.sunk | while | flops 100679680 | bytes 1443397 | solution.py:43
  77.9 2.9 bitcast_dynamic-update-slice_fusion.5
  80.8 2.9 bitcast_dynamic-update-slice_fusion.5
  83.8 2.9 bitcast_dynamic-update-slice_fusion.5
  86.7 2.9 bitcast_dynamic-update-slice_fusion.5
  89.6 1.9 collective-permute-start.1
  92.6 4.1 collective-permute-done.1
  97.4 12.0 %collective-permute-start.1 = (f32[512,32]{0,1:T(8,128)S(1)}, f32[512,32]{0,1:T(8,128)S(1)}, u32[]{:S(2)}, u32[]{:S(2)}) collective-permute-start(f32[512,32]{0,1:T(8,128)S(1)} %get-tuple-element.643), channel_id=1, source_target_pairs={{0,4},{4,8},{8,12},{12,16},{16,20},{20,24},{24,28},{1,5},{5,9},{9,... | collective-permute-start | bytes 196616 | tf_op jit(solution)/shard_map/while/body/eval_jaxpr/ppermute | solution.py:23
  109.5 1.8 collective-permute-done.1
  112.0 4.3 collective-permute-start.1
  116.4 2.7 collective-permute-done.1
  119.8 12.9 %collective-permute-start.1 = (f32[512,32]{0,1:T(8,128)S(1)}, f32[512,32]{0,1:T(8,128)S(1)}, u32[]{:S(2)}, u32[]{:S(2)}) collective-permute-start(f32[512,32]{0,1:T(8,128)S(1)} %get-tuple-element.643), channel_id=1, source_target_pairs={{0,4},{4,8},{8,12},{12,16},{16,20},{20,24},{24,28},{1,5},{5,9},{9,... | collective-permute-start | bytes 196616 | tf_op jit(solution)/shard_map/while/body/eval_jaxpr/ppermute | solution.py:23
  135.3 5.2 %collective-permute-start.1 = (f32[512,32]{0,1:T(8,128)S(1)}, f32[512,32]{0,1:T(8,128)S(1)}, u32[]{:S(2)}, u32[]{:S(2)}) collective-permute-start(f32[512,32]{0,1:T(8,128)S(1)} %get-tuple-element.643), channel_id=1, source_target_pairs={{0,4},{4,8},{8,12},{12,16},{16,20},{20,24},{24,28},{1,5},{5,9},{9,... | collective-permute-start | bytes 196616 | tf_op jit(solution)/shard_map/while/body/eval_jaxpr/ppermute | solution.py:23
  143.1 12.0 %collective-permute-start.1 = (f32[512,32]{0,1:T(8,128)S(1)}, f32[512,32]{0,1:T(8,128)S(1)}, u32[]{:S(2)}, u32[]{:S(2)}) collective-permute-start(f32[512,32]{0,1:T(8,128)S(1)} %get-tuple-element.643), channel_id=1, source_target_pairs={{0,4},{4,8},{8,12},{12,16},{16,20},{20,24},{24,28},{1,5},{5,9},{9,... | collective-permute-start | bytes 196616 | tf_op jit(solution)/shard_map/while/body/eval_jaxpr/ppermute | solution.py:23
  157.0 155.7 %while.61 = (s32[]{:T(128)}, f32[4,512,32]{1,2,0:T(8,128)S(1)}, f32[512,32]{0,1:T(8,128)S(1)}, s32[]{:T(128)}, f32[4,512,32]{1,2,0:T(8,128)S(1)}, /*index=5*/f32[4,512,512]{2,1,0:T(8,128)}, s32[]{:T(128)}, s32[]{:T(128)}) while((s32[]{:T(128)}, f32[4,512,32]{1,2,0:T(8,128)S(1)}, f32[512,32]{0,1:T(8,128)S(1)}, s32[]{:T(128)}, ...), condition=%wide.region_13.14_spmd.clone, body=%wide.region_8.13_spmd.clone.sunk | while | flops 100810760 | bytes 2884979 | solution.py:79
  157.7 1.9 collective-permute-start
  159.8 5.4 %collective-permute-done = f32[512,32]{0,1:T(8,128)S(1)} collective-permute-done((f32[512,32]{0,1:T(8,128)S(1)}, f32[512,32]{0,1:T(8,128)S(1)}, u32[]{:S(2)}, u32[]{:S(2)}) %collective-permute-start) | collective-permute-done | bytes 65568 | tf_op jit(solution)/shard_map/while/body/eval_jaxpr/ppermute | solution.py:23
  165.9 2.2 collective-permute-start
  168.2 13.4 %collective-permute-done = f32[512,32]{0,1:T(8,128)S(1)} collective-permute-done((f32[512,32]{0,1:T(8,128)S(1)}, f32[512,32]{0,1:T(8,128)S(1)}, u32[]{:S(2)}, u32[]{:S(2)}) %collective-permute-start) | collective-permute-done | bytes 65568 | tf_op jit(solution)/shard_map/while/body/eval_jaxpr/ppermute | solution.py:23
  182.4 1.9 collective-permute-start
  184.4 5.0 %collective-permute-done = f32[512,32]{0,1:T(8,128)S(1)} collective-permute-done((f32[512,32]{0,1:T(8,128)S(1)}, f32[512,32]{0,1:T(8,128)S(1)}, u32[]{:S(2)}, u32[]{:S(2)}) %collective-permute-start) | collective-permute-done | bytes 65568 | tf_op jit(solution)/shard_map/while/body/eval_jaxpr/ppermute | solution.py:23
  190.1 1.9 collective-permute-start
  192.2 11.9 %collective-permute-done = f32[512,32]{0,1:T(8,128)S(1)} collective-permute-done((f32[512,32]{0,1:T(8,128)S(1)}, f32[512,32]{0,1:T(8,128)S(1)}, u32[]{:S(2)}, u32[]{:S(2)}) %collective-permute-start) | collective-permute-done | bytes 65568 | tf_op jit(solution)/shard_map/while/body/eval_jaxpr/ppermute | solution.py:23
  204.8 1.9 collective-permute-start
  206.9 62.3 %collective-permute-done = f32[512,32]{0,1:T(8,128)S(1)} collective-permute-done((f32[512,32]{0,1:T(8,128)S(1)}, f32[512,32]{0,1:T(8,128)S(1)}, u32[]{:S(2)}, u32[]{:S(2)}) %collective-permute-start) | collective-permute-done | bytes 65568 | tf_op jit(solution)/shard_map/while/body/eval_jaxpr/ppermute | solution.py:23
  269.2 12.4 %conditional.7 = (f32[512,32]{0,1:T(8,128)S(1)}, f32[4,512,32]{1,2,0:T(8,128)}) conditional(s32[]{:T(128)} %convert_element_type.27, () %tuple.153, (f32[4,512,32]{1,2,0:T(8,128)S(1)}, f32[4,512,512]{2,1,0:T(8,128)}, f32[512,32]{0,1:T(8,128)S(1)}) %tuple.154), branch_computations={%region_9.9_spmd, %region_10.12_spmd} | conditional | flops 100679680 | bytes 1836205 | solution.py:74
  270.0 11.7 %while.59 = (s32[]{:T(128)}, f32[512,32]{0,1:T(8,128)S(1)}, f32[4,512,32]{1,2,0:T(8,128)}, f32[4,512,32]{1,2,0:T(8,128)S(1)}, f32[4,512,512]{2,1,0:T(8,128)}, /*index=5*/s32[]{:T(128)}, s32[]{:T(128)}) while((s32[]{:T(128)}, f32[512,32]{0,1:T(8,128)S(1)}, f32[4,512,32]{1,2,0:T(8,128)}, f32[4,512,32]{1,2,0:T(8,128)S(1)}, ...), condition=%wide.region_12.11_spmd, body=%wide.region_11.10_spmd.sunk | while | flops 100679680 | bytes 1442905 | solution.py:53
  270.0 2.9 bitcast_dynamic-update-slice_fusion.4
  272.9 2.9 bitcast_dynamic-update-slice_fusion.4
  275.8 2.9 bitcast_dynamic-update-slice_fusion.4
  278.7 2.9 bitcast_dynamic-update-slice_fusion.4
  281.7 1.9 collective-permute-start
  284.6 3.2 collective-permute-done
  288.5 14.5 %collective-permute-start = (f32[512,32]{0,1:T(8,128)S(1)}, f32[512,32]{0,1:T(8,128)S(1)}, u32[]{:S(2)}, u32[]{:S(2)}) collective-permute-start(f32[512,32]{0,1:T(8,128)S(1)} %get-tuple-element.651), channel_id=1, source_target_pairs={{4,0},{8,4},{12,8},{16,12},{20,16},{24,20},{28,24},{5,1},{9,5},{13... | collective-permute-start | bytes 196616 | tf_op jit(solution)/shard_map/while/body/eval_jaxpr/ppermute | solution.py:23
  305.7 5.2 %collective-permute-start = (f32[512,32]{0,1:T(8,128)S(1)}, f32[512,32]{0,1:T(8,128)S(1)}, u32[]{:S(2)}, u32[]{:S(2)}) collective-permute-start(f32[512,32]{0,1:T(8,128)S(1)} %get-tuple-element.651), channel_id=1, source_target_pairs={{4,0},{8,4},{12,8},{16,12},{20,16},{24,20},{28,24},{5,1},{9,5},{13... | collective-permute-start | bytes 196616 | tf_op jit(solution)/shard_map/while/body/eval_jaxpr/ppermute | solution.py:23
  314.5 5.1 %all-to-all-start.1 = ((f32[4,1,16384]{2,1,0:T(1,128)}), f32[4,1,16384]{2,1,0:T(1,128)S(1)}, u32[]{:S(2)}, u32[]{:S(2)}) async-start(f32[4,1,16384]{2,1,0:T(1,128)} %reshape.6), calls=%async_computation.1 | async-start | bytes 524288 | tf_op jit(solution)/shard_map/all_to_all | solution.py:103
  319.6 4.3 all-to-all-done.1
  326.8 12.7 %collective-permute-start.2 = (f32[1,128,128]{1,2,0:T(8,128)S(1)}, f32[1,128,128]{1,2,0:T(8,128)S(1)}, u32[]{:S(2)}, u32[]{:S(2)}) collective-permute-start(f32[1,128,128]{1,2,0:T(8,128)S(1)} %bitcast.60), channel_id=1, source_target_pairs={{4,0},{8,4},{12,8},{16,12},{20,16},{24,20},{28,24},{5,1},{9,5},{13... | collective-permute-start | bytes 196616 | tf_op jit(solution)/shard_map/ppermute | solution.py:15
  339.5 1.9 collective-permute-start.3
  341.8 4.7 %collective-permute-done.3 = f32[1,128,128]{1,2,0:T(8,128)S(1)} collective-permute-done((f32[1,128,128]{1,2,0:T(8,128)S(1)}, f32[1,128,128]{1,2,0:T(8,128)S(1)}, u32[]{:S(2)}, u32[]{:S(2)}) %collective-permute-start.3) | collective-permute-done | bytes 65568 | tf_op jit(solution)/shard_map/ppermute | solution.py:14
  346.8 1.9 collective-permute-start.4
  348.7 2.4 collective-permute-start.5
  351.2 2.8 collective-permute-done.4
  354.0 3.8 collective-permute-done.5
  358.1 3.4 collective-permute-start.10
  361.5 2.5 collective-permute-start.11
  364.1 1.9 collective-permute-start.8
  366.1 2.4 collective-permute-start.9
  368.8 3.1 collective-permute-start.12
  371.9 1.9 collective-permute-start.13
  375.2 2.0 collective-permute-done.12
  377.2 3.8 collective-permute-done.13
  383.4 41.7 %all-reduce.6 = (f32[]{:T(128)}, f32[]{:T(128)}, f32[]{:T(128)}, f32[]{:T(128)}, f32[]{:T(128)}, /*index=5*/f32[]{:T(128)}, f32[]{:T(128)}, f32[]{:T(128)}) all-reduce(f32[]{:T(128)} %get-tuple-element.434, f32[]{:T(128)} %multiply_reduce_fusion.8, f32[]{:T(128)} %get-tuple-element.433, ...), channel_id=1, replica_groups=mesh['layer'=8,'split'=4] {'layer','split'}, use_global_device_ids=true, to_apply=%region_17.18 | all-reduce | flops 8 | bytes 64 | tf_op jit(solution)/shard_map/psum | solution.py:106
  (120 shorter events, 48.6 us)
Async XLA Ops:
  7.2 37.6 %all-gather.2.cloned.1.call-start = ((), (), s32[]{:S(2)}) async-start(), calls=%async_computation.2 | async-start | bytes 5242880 | tf_op jit(solution)/shard_map/all_gather | solution.py:86
  9.7 13.7 %all-to-all-start = ((f32[4,128,128]{1,0,2:T(4,128)}), f32[4,128,128]{1,0,2:T(4,128)S(1)}, u32[]{:S(2)}, u32[]{:S(2)}) async-start(f32[4,128,128]{1,0,2:T(4,128)} %copy.44), calls=%async_computation | async-start | bytes 524288 | tf_op jit(solution)/shard_map/all_to_all | solution.py:87
  14.7 326.8 %collective-permute-start.6 = (f32[1,128,128]{1,2,0:T(8,128)S(1)}, f32[1,128,128]{1,2,0:T(8,128)S(1)}, u32[]{:S(2)}, u32[]{:S(2)}) collective-permute-start(f32[1,128,128]{1,2,0:T(8,128)S(1)} %get-tuple-element.507), channel_id=1, source_target_pairs={{4,0},{8,4},{12,8},{16,12},{20,16},{24,20},{28,24},{5,1},{9,5},{13... | collective-permute-start | bytes 196616 | tf_op jit(solution)/shard_map/ppermute | solution.py:15
  18.0 323.5 %collective-permute-start.7 = (f32[1,128,128]{1,2,0:T(8,128)S(1)}, f32[1,128,128]{1,2,0:T(8,128)S(1)}, u32[]{:S(2)}, u32[]{:S(2)}) collective-permute-start(f32[1,128,128]{1,2,0:T(8,128)S(1)} %get-tuple-element.506), channel_id=1, source_target_pairs={{0,4},{4,8},{8,12},{12,16},{16,20},{20,24},{24,28},{1,5},{5,9},{9,... | collective-permute-start | bytes 196616 | tf_op jit(solution)/shard_map/ppermute | solution.py:14
  45.5 7.0 %collective-permute-start.1 = (f32[512,32]{0,1:T(8,128)S(1)}, f32[512,32]{0,1:T(8,128)S(1)}, u32[]{:S(2)}, u32[]{:S(2)}) collective-permute-start(f32[512,32]{0,1:T(8,128)S(1)} %get-tuple-element.643), channel_id=1, source_target_pairs={{0,4},{4,8},{8,12},{12,16},{16,20},{20,24},{24,28},{1,5},{5,9},{9,... | collective-permute-start | bytes 196616 | tf_op jit(solution)/shard_map/while/body/eval_jaxpr/ppermute | solution.py:23
  53.3 24.6 %collective-permute-start.1 = (f32[512,32]{0,1:T(8,128)S(1)}, f32[512,32]{0,1:T(8,128)S(1)}, u32[]{:S(2)}, u32[]{:S(2)}) collective-permute-start(f32[512,32]{0,1:T(8,128)S(1)} %get-tuple-element.643), channel_id=1, source_target_pairs={{0,4},{4,8},{8,12},{12,16},{16,20},{20,24},{24,28},{1,5},{5,9},{9,... | collective-permute-start | bytes 196616 | tf_op jit(solution)/shard_map/while/body/eval_jaxpr/ppermute | solution.py:23
  89.6 7.1 %collective-permute-start.1 = (f32[512,32]{0,1:T(8,128)S(1)}, f32[512,32]{0,1:T(8,128)S(1)}, u32[]{:S(2)}, u32[]{:S(2)}) collective-permute-start(f32[512,32]{0,1:T(8,128)S(1)} %get-tuple-element.643), channel_id=1, source_target_pairs={{0,4},{4,8},{8,12},{12,16},{16,20},{20,24},{24,28},{1,5},{5,9},{9,... | collective-permute-start | bytes 196616 | tf_op jit(solution)/shard_map/while/body/eval_jaxpr/ppermute | solution.py:23
  97.4 13.9 %collective-permute-start.1 = (f32[512,32]{0,1:T(8,128)S(1)}, f32[512,32]{0,1:T(8,128)S(1)}, u32[]{:S(2)}, u32[]{:S(2)}) collective-permute-start(f32[512,32]{0,1:T(8,128)S(1)} %get-tuple-element.643), channel_id=1, source_target_pairs={{0,4},{4,8},{8,12},{12,16},{16,20},{20,24},{24,28},{1,5},{5,9},{9,... | collective-permute-start | bytes 196616 | tf_op jit(solution)/shard_map/while/body/eval_jaxpr/ppermute | solution.py:23
  112.0 7.0 %collective-permute-start.1 = (f32[512,32]{0,1:T(8,128)S(1)}, f32[512,32]{0,1:T(8,128)S(1)}, u32[]{:S(2)}, u32[]{:S(2)}) collective-permute-start(f32[512,32]{0,1:T(8,128)S(1)} %get-tuple-element.643), channel_id=1, source_target_pairs={{0,4},{4,8},{8,12},{12,16},{16,20},{20,24},{24,28},{1,5},{5,9},{9,... | collective-permute-start | bytes 196616 | tf_op jit(solution)/shard_map/while/body/eval_jaxpr/ppermute | solution.py:23
  119.8 14.8 %collective-permute-start.1 = (f32[512,32]{0,1:T(8,128)S(1)}, f32[512,32]{0,1:T(8,128)S(1)}, u32[]{:S(2)}, u32[]{:S(2)}) collective-permute-start(f32[512,32]{0,1:T(8,128)S(1)} %get-tuple-element.643), channel_id=1, source_target_pairs={{0,4},{4,8},{8,12},{12,16},{16,20},{20,24},{24,28},{1,5},{5,9},{9,... | collective-permute-start | bytes 196616 | tf_op jit(solution)/shard_map/while/body/eval_jaxpr/ppermute | solution.py:23
  135.3 7.0 %collective-permute-start.1 = (f32[512,32]{0,1:T(8,128)S(1)}, f32[512,32]{0,1:T(8,128)S(1)}, u32[]{:S(2)}, u32[]{:S(2)}) collective-permute-start(f32[512,32]{0,1:T(8,128)S(1)} %get-tuple-element.643), channel_id=1, source_target_pairs={{0,4},{4,8},{8,12},{12,16},{16,20},{20,24},{24,28},{1,5},{5,9},{9,... | collective-permute-start | bytes 196616 | tf_op jit(solution)/shard_map/while/body/eval_jaxpr/ppermute | solution.py:23
  143.1 13.9 %collective-permute-start.1 = (f32[512,32]{0,1:T(8,128)S(1)}, f32[512,32]{0,1:T(8,128)S(1)}, u32[]{:S(2)}, u32[]{:S(2)}) collective-permute-start(f32[512,32]{0,1:T(8,128)S(1)} %get-tuple-element.643), channel_id=1, source_target_pairs={{0,4},{4,8},{8,12},{12,16},{16,20},{20,24},{24,28},{1,5},{5,9},{9,... | collective-permute-start | bytes 196616 | tf_op jit(solution)/shard_map/while/body/eval_jaxpr/ppermute | solution.py:23
  157.7 7.4 %collective-permute-start = (f32[512,32]{0,1:T(8,128)S(1)}, f32[512,32]{0,1:T(8,128)S(1)}, u32[]{:S(2)}, u32[]{:S(2)}) collective-permute-start(f32[512,32]{0,1:T(8,128)S(1)} %get-tuple-element.651), channel_id=1, source_target_pairs={{4,0},{8,4},{12,8},{16,12},{20,16},{24,20},{28,24},{5,1},{9,5},{13... | collective-permute-start | bytes 196616 | tf_op jit(solution)/shard_map/while/body/eval_jaxpr/ppermute | solution.py:23
  165.9 15.7 %collective-permute-start = (f32[512,32]{0,1:T(8,128)S(1)}, f32[512,32]{0,1:T(8,128)S(1)}, u32[]{:S(2)}, u32[]{:S(2)}) collective-permute-start(f32[512,32]{0,1:T(8,128)S(1)} %get-tuple-element.651), channel_id=1, source_target_pairs={{4,0},{8,4},{12,8},{16,12},{20,16},{24,20},{28,24},{5,1},{9,5},{13... | collective-permute-start | bytes 196616 | tf_op jit(solution)/shard_map/while/body/eval_jaxpr/ppermute | solution.py:23
  182.4 7.0 %collective-permute-start = (f32[512,32]{0,1:T(8,128)S(1)}, f32[512,32]{0,1:T(8,128)S(1)}, u32[]{:S(2)}, u32[]{:S(2)}) collective-permute-start(f32[512,32]{0,1:T(8,128)S(1)} %get-tuple-element.651), channel_id=1, source_target_pairs={{4,0},{8,4},{12,8},{16,12},{20,16},{24,20},{28,24},{5,1},{9,5},{13... | collective-permute-start | bytes 196616 | tf_op jit(solution)/shard_map/while/body/eval_jaxpr/ppermute | solution.py:23
  190.1 14.0 %collective-permute-start = (f32[512,32]{0,1:T(8,128)S(1)}, f32[512,32]{0,1:T(8,128)S(1)}, u32[]{:S(2)}, u32[]{:S(2)}) collective-permute-start(f32[512,32]{0,1:T(8,128)S(1)} %get-tuple-element.651), channel_id=1, source_target_pairs={{4,0},{8,4},{12,8},{16,12},{20,16},{24,20},{28,24},{5,1},{9,5},{13... | collective-permute-start | bytes 196616 | tf_op jit(solution)/shard_map/while/body/eval_jaxpr/ppermute | solution.py:23
  204.8 64.4 %collective-permute-start = (f32[512,32]{0,1:T(8,128)S(1)}, f32[512,32]{0,1:T(8,128)S(1)}, u32[]{:S(2)}, u32[]{:S(2)}) collective-permute-start(f32[512,32]{0,1:T(8,128)S(1)} %get-tuple-element.651), channel_id=1, source_target_pairs={{4,0},{8,4},{12,8},{16,12},{20,16},{24,20},{28,24},{5,1},{9,5},{13... | collective-permute-start | bytes 196616 | tf_op jit(solution)/shard_map/while/body/eval_jaxpr/ppermute | solution.py:23
  281.7 6.2 %collective-permute-start = (f32[512,32]{0,1:T(8,128)S(1)}, f32[512,32]{0,1:T(8,128)S(1)}, u32[]{:S(2)}, u32[]{:S(2)}) collective-permute-start(f32[512,32]{0,1:T(8,128)S(1)} %get-tuple-element.651), channel_id=1, source_target_pairs={{4,0},{8,4},{12,8},{16,12},{20,16},{24,20},{28,24},{5,1},{9,5},{13... | collective-permute-start | bytes 196616 | tf_op jit(solution)/shard_map/while/body/eval_jaxpr/ppermute | solution.py:23
  288.5 16.4 %collective-permute-start = (f32[512,32]{0,1:T(8,128)S(1)}, f32[512,32]{0,1:T(8,128)S(1)}, u32[]{:S(2)}, u32[]{:S(2)}) collective-permute-start(f32[512,32]{0,1:T(8,128)S(1)} %get-tuple-element.651), channel_id=1, source_target_pairs={{4,0},{8,4},{12,8},{16,12},{20,16},{24,20},{28,24},{5,1},{9,5},{13... | collective-permute-start | bytes 196616 | tf_op jit(solution)/shard_map/while/body/eval_jaxpr/ppermute | solution.py:23
  305.7 7.0 %collective-permute-start = (f32[512,32]{0,1:T(8,128)S(1)}, f32[512,32]{0,1:T(8,128)S(1)}, u32[]{:S(2)}, u32[]{:S(2)}) collective-permute-start(f32[512,32]{0,1:T(8,128)S(1)} %get-tuple-element.651), channel_id=1, source_target_pairs={{4,0},{8,4},{12,8},{16,12},{20,16},{24,20},{28,24},{5,1},{9,5},{13... | collective-permute-start | bytes 196616 | tf_op jit(solution)/shard_map/while/body/eval_jaxpr/ppermute | solution.py:23
  314.5 9.4 %all-to-all-start.1 = ((f32[4,1,16384]{2,1,0:T(1,128)}), f32[4,1,16384]{2,1,0:T(1,128)S(1)}, u32[]{:S(2)}, u32[]{:S(2)}) async-start(f32[4,1,16384]{2,1,0:T(1,128)} %reshape.6), calls=%async_computation.1 | async-start | bytes 524288 | tf_op jit(solution)/shard_map/all_to_all | solution.py:103
  326.8 15.1 %collective-permute-start.2 = (f32[1,128,128]{1,2,0:T(8,128)S(1)}, f32[1,128,128]{1,2,0:T(8,128)S(1)}, u32[]{:S(2)}, u32[]{:S(2)}) collective-permute-start(f32[1,128,128]{1,2,0:T(8,128)S(1)} %bitcast.60), channel_id=1, source_target_pairs={{4,0},{8,4},{12,8},{16,12},{20,16},{24,20},{28,24},{5,1},{9,5},{13... | collective-permute-start | bytes 196616 | tf_op jit(solution)/shard_map/ppermute | solution.py:15
  339.5 7.1 %collective-permute-start.3 = (f32[1,128,128]{1,2,0:T(8,128)S(1)}, f32[1,128,128]{1,2,0:T(8,128)S(1)}, u32[]{:S(2)}, u32[]{:S(2)}) collective-permute-start(f32[1,128,128]{1,2,0:T(8,128)S(1)} %bitcast.61), channel_id=1, source_target_pairs={{0,4},{4,8},{8,12},{12,16},{16,20},{20,24},{24,28},{1,5},{5,9},{9,... | collective-permute-start | bytes 196616 | tf_op jit(solution)/shard_map/ppermute | solution.py:14
  346.8 7.2 %collective-permute-start.4 = (f32[6,1,128]{1,2,0:T(8,128)S(1)}, f32[6,1,128]{1,2,0:T(8,128)S(1)}, u32[]{:S(2)}, u32[]{:S(2)}) collective-permute-start(f32[6,1,128]{1,2,0:T(8,128)S(1)} %get-tuple-element.500), channel_id=1, source_target_pairs={{1,0},{2,1},{3,2},{5,4},{6,5},{7,6},{9,8},{10,9},{11,10},{13,12},{... | collective-permute-start | bytes 9224 | tf_op jit(solution)/shard_map/ppermute | solution.py:15
  348.7 9.1 %collective-permute-start.5 = (f32[6,1,128]{1,2,0:T(8,128)S(1)}, f32[6,1,128]{1,2,0:T(8,128)S(1)}, u32[]{:S(2)}, u32[]{:S(2)}) collective-permute-start(f32[6,1,128]{1,2,0:T(8,128)S(1)} %get-tuple-element.501), channel_id=1, source_target_pairs={{0,1},{1,2},{2,3},{4,5},{5,6},{6,7},{8,9},{9,10},{10,11},{12,13},{... | collective-permute-start | bytes 9224 | tf_op jit(solution)/shard_map/ppermute | solution.py:14
  358.1 10.4 %collective-permute-start.10 = (f32[1,128,128]{1,2,0:T(8,128)S(1)}, f32[1,128,128]{1,2,0:T(8,128)S(1)}, u32[]{:S(2)}, u32[]{:S(2)}) collective-permute-start(f32[1,128,128]{1,2,0:T(8,128)S(1)} %get-tuple-element.503), channel_id=1, source_target_pairs={{4,0},{8,4},{12,8},{16,12},{20,16},{24,20},{28,24},{5,1},{9,5},{13... | collective-permute-start | bytes 196616 | tf_op jit(solution)/shard_map/ppermute | solution.py:15
  361.5 7.1 %collective-permute-start.11 = (f32[1,128,128]{1,2,0:T(8,128)S(1)}, f32[1,128,128]{1,2,0:T(8,128)S(1)}, u32[]{:S(2)}, u32[]{:S(2)}) collective-permute-start(f32[1,128,128]{1,2,0:T(8,128)S(1)} %get-tuple-element.502), channel_id=1, source_target_pairs={{0,4},{4,8},{8,12},{12,16},{16,20},{20,24},{24,28},{1,5},{5,9},{9,... | collective-permute-start | bytes 196616 | tf_op jit(solution)/shard_map/ppermute | solution.py:14
  364.1 9.7 %collective-permute-start.8 = (f32[6,1,128]{1,2,0:T(8,128)S(1)}, f32[6,1,128]{1,2,0:T(8,128)S(1)}, u32[]{:S(2)}, u32[]{:S(2)}) collective-permute-start(f32[6,1,128]{1,2,0:T(8,128)S(1)} %get-tuple-element.498), channel_id=1, source_target_pairs={{1,0},{2,1},{3,2},{5,4},{6,5},{7,6},{9,8},{10,9},{11,10},{13,12},{... | collective-permute-start | bytes 9224 | tf_op jit(solution)/shard_map/ppermute | solution.py:15
  366.1 9.1 %collective-permute-start.9 = (f32[6,1,128]{1,2,0:T(8,128)S(1)}, f32[6,1,128]{1,2,0:T(8,128)S(1)}, u32[]{:S(2)}, u32[]{:S(2)}) collective-permute-start(f32[6,1,128]{1,2,0:T(8,128)S(1)} %get-tuple-element.499), channel_id=1, source_target_pairs={{0,1},{1,2},{2,3},{4,5},{5,6},{6,7},{8,9},{9,10},{10,11},{12,13},{... | collective-permute-start | bytes 9224 | tf_op jit(solution)/shard_map/ppermute | solution.py:14
  368.8 8.4 %collective-permute-start.12 = (f32[6,1,128]{1,2,0:T(8,128)S(1)}, f32[6,1,128]{1,2,0:T(8,128)S(1)}, u32[]{:S(2)}, u32[]{:S(2)}) collective-permute-start(f32[6,1,128]{1,2,0:T(8,128)S(1)} %get-tuple-element.496), channel_id=1, source_target_pairs={{1,0},{2,1},{3,2},{5,4},{6,5},{7,6},{9,8},{10,9},{11,10},{13,12},{... | collective-permute-start | bytes 9224 | tf_op jit(solution)/shard_map/ppermute | solution.py:15
  371.9 9.1 %collective-permute-start.13 = (f32[6,1,128]{1,2,0:T(8,128)S(1)}, f32[6,1,128]{1,2,0:T(8,128)S(1)}, u32[]{:S(2)}, u32[]{:S(2)}) collective-permute-start(f32[6,1,128]{1,2,0:T(8,128)S(1)} %get-tuple-element.497), channel_id=1, source_target_pairs={{0,1},{1,2},{2,3},{4,5},{5,6},{6,7},{8,9},{9,10},{10,11},{12,13},{... | collective-permute-start | bytes 9224 | tf_op jit(solution)/shard_map/ppermute | solution.py:14
Sparse Core Ops, SparseCore 0:
  9.5 35.1 all-gather.1
where the time goes:
time: 441 us; the launch traced here: 439 us
  waiting for transfers between devices  189 us (43%)
  starting transfers between devices  134 us (30%)
  blocking collectives  41.7 us (9%)
  matrix products  23.3 us (5%)
  local copies, waits for them, and re-layouts  20.9 us (5%)
  between operations  20.8 us (5%)
  other arithmetic  8.15 us (2%)
    ppermute x16, waiting for transfers between devices, from_behind(): return lax.ppermute(block, axis, route)  144 us
    ppermute x16, starting transfers between devices, from_behind(): return lax.ppermute(block, axis, route)  85.4 us
    psum x1, blocking collectives, per_device(): lax.psum((jnp.sum(right_side * right_side), jnp.sum(right_side * image),...  41.7 us
    ppermute x6, starting transfers between devices, with_halo(): after = lax.ppermute(first, axis, down)  26.3 us
    all_gather x1, waiting for transfers between devices, per_device(): matrices = lax.all_gather(inverses, 'split', axis=2, tiled=True)  21.4 us
    ppermute x6, starting transfers between devices, with_halo(): before = lax.ppermute(last, axis, up)  13.7 us
    ppermute x6, waiting for transfers between devices, with_halo(): before = lax.ppermute(last, axis, up)  13.7 us
    dot_general x4, matrix products, down_advance(): state = jnp.dot(matrix, source + state, precision=lax.Precision.HIGHEST)  11.7 us
  transfers between devices with their start and end apart: 31, of which 24 were waited for; matrix products, arithmetic and copies ran while one was open for 11% of the time, Pallas kernels for 0%

commit v1 on v0

--- a/solution.py
+++ b/solution.py
@@ -104,18 +104,21 @@
     image = stencil(direction, diagonal)
     applied_image = stencil(image, diagonal)
     sums_all = lax.psum(
-        (
-            jnp.sum(right_side * right_side),
-            jnp.sum(right_side * image),
-            jnp.sum(applied_rhs * right_side),
-            jnp.sum(applied_rhs * image),
-            jnp.sum(applied_image * right_side),
-            jnp.sum(applied_image * image),
-            jnp.sum(applied_rhs * applied_rhs),
-            jnp.sum(applied_rhs * applied_image),
-            jnp.sum(applied_image * applied_image),
+        lax.psum(
+            (
+                jnp.sum(right_side * right_side),
+                jnp.sum(right_side * image),
+                jnp.sum(applied_rhs * right_side),
+                jnp.sum(applied_rhs * image),
+                jnp.sum(applied_image * right_side),
+                jnp.sum(applied_image * image),
+                jnp.sum(applied_rhs * applied_rhs),
+                jnp.sum(applied_rhs * applied_image),
+                jnp.sum(applied_image * applied_image),
+            ),
+            "split",
         ),
-        ("layer", "split"),
+        "layer",
     )
     (
         norm_sq,

time: 441 us -> 426 us (0.966)
  blocking collectives: 41.7 us -> 24 us
    psum x1, blocking collectives: 41.7 us -> 6.49 us  [per_device(): lax.psum((jnp.sum(right_side * right_side), jnp.sum(right_side * image),...]
    psum x0 -> x1, blocking collectives: none -> 17.5 us  [per_device(): lax.psum(lax.psum((jnp.sum(right_side * right_side), jnp.sum(right_side *...]
  transfers between devices with their start and end apart: 31 -> 31, of which waited for: 24 -> 24; matrix products, arithmetic and copies ran while one was open for 11% -> 12% of each run, Pallas kernels for 0% -> 0%
where the time goes in v1:
time: 426 us; the launch traced here: 421 us
  waiting for transfers between devices  189 us (44%)
  starting transfers between devices  134 us (31%)
  blocking collectives  24 us (6%)
  matrix products  23.3 us (5%)
  local copies, waits for them, and re-layouts  20.9 us (5%)
  between operations  20.7 us (5%)
  other arithmetic  8.09 us (2%)
    ppermute x16, waiting for transfers between devices, from_behind(): return lax.ppermute(block, axis, route)  144 us
    ppermute x16, starting transfers between devices, from_behind(): return lax.ppermute(block, axis, route)  85.4 us
    ppermute x6, starting transfers between devices, with_halo(): after = lax.ppermute(first, axis, down)  26.3 us
    all_gather x1, waiting for transfers between devices, per_device(): matrices = lax.all_gather(inverses, 'split', axis=2, tiled=True)  21.4 us
    psum x1, blocking collectives, per_device(): lax.psum(lax.psum((jnp.sum(right_side * right_side), jnp.sum(right_side *...  17.5 us
    ppermute x6, starting transfers between devices, with_halo(): before = lax.ppermute(last, axis, up)  13.7 us
    ppermute x6, waiting for transfers between devices, with_halo(): before = lax.ppermute(last, axis, up)  13.7 us
    dot_general x4, matrix products, down_advance(): state = jnp.dot(matrix, source + state, precision=lax.Precision.HIGHEST)  11.7 us
  transfers between devices with their start and end apart: 31, of which 24 were waited for; matrix products, arithmetic and copies ran while one was open for 12% of the time, Pallas kernels for 0%

profile of v1, /device:TPU:12, one launch (start us, length us, event | category | flops | bytes accessed | tf_op | source)
XLA Modules:
  0.0 421.2 jit_solution(15041742059451401053)
XLA Ops:
  7.9 1.8 copy.44
  9.7 3.9 all-to-all-start
  14.7 3.3 collective-permute-start.6
  18.0 2.6 collective-permute-start.7
  23.3 21.4 %all-gather.2.cloned.1.call-done = f32[4,512,512]{2,1,0:T(8,128)} async-done(((f32[4,512,128]{2,1,0:T(8,128)}), f32[4,512,512]{2,1,0:T(8,128)}) %all-gather.2.cloned.1.call-update) | async-done | bytes 4194320 | tf_op jit(solution)/shard_map/all_gather | solution.py:86
  44.8 112.2 %while.60 = (s32[]{:T(128)}, f32[4,512,32]{1,2,0:T(8,128)S(1)}, f32[512,32]{0,1:T(8,128)S(1)}, s32[]{:T(128)}, f32[4,512,512]{2,1,0:T(8,128)}, /*index=5*/f32[4,512,32]{1,2,0:T(8,128)S(1)}, s32[]{:T(128)}, s32[]{:T(128)}) while((s32[]{:T(128)}, f32[4,512,32]{1,2,0:T(8,128)S(1)}, f32[512,32]{0,1:T(8,128)S(1)}, s32[]{:T(128)}, ...), condition=%wide.region_8.9_spmd.clone, body=%wide.region_3.8_spmd.clone.sunk | while | flops 100810760 | bytes 2623315 | solution.py:79
  45.5 3.4 collective-permute-start.1
  49.0 3.6 collective-permute-done.1
  53.3 2.5 collective-permute-start.1
  55.9 22.0 %collective-permute-done.1 = f32[512,32]{0,1:T(8,128)S(1)} collective-permute-done((f32[512,32]{0,1:T(8,128)S(1)}, f32[512,32]{0,1:T(8,128)S(1)}, u32[]{:S(2)}, u32[]{:S(2)}) %collective-permute-start.1) | collective-permute-done | bytes 65568 | tf_op jit(solution)/shard_map/while/body/eval_jaxpr/ppermute | solution.py:23
  77.9 11.7 %conditional.6 = (f32[512,32]{0,1:T(8,128)S(1)}, f32[4,512,32]{1,2,0:T(8,128)}) conditional(s32[]{:T(128)} %convert_element_type.26, () %tuple.150, (f32[4,512,512]{2,1,0:T(8,128)}, f32[4,512,32]{1,2,0:T(8,128)S(1)}, f32[512,32]{0,1:T(8,128)S(1)}) %tuple.151), branch_computations={%region_4.4_spmd, %region_5.7_spmd} | conditional | flops 100679680 | bytes 1574541 | solution.py:74
  77.9 11.7 %while.58 = (s32[]{:T(128)}, f32[512,32]{0,1:T(8,128)S(1)}, f32[4,512,32]{1,2,0:T(8,128)}, f32[4,512,512]{2,1,0:T(8,128)}, f32[4,512,32]{1,2,0:T(8,128)S(1)}, /*index=5*/s32[]{:T(128)}) while((s32[]{:T(128)}, f32[512,32]{0,1:T(8,128)S(1)}, f32[4,512,32]{1,2,0:T(8,128)}, f32[4,512,512]{2,1,0:T(8,128)}, f32[4,512,32]{1,2,0:T(8,128)S(1)}, ...), condition=%wide.region_7.6_spmd, body=%wide.region_6.5_spmd.sunk | while | flops 100679680 | bytes 1443397 | solution.py:43
  77.9 2.9 bitcast_dynamic-update-slice_fusion.5
  80.8 2.9 bitcast_dynamic-update-slice_fusion.5
  83.8 2.9 bitcast_dynamic-update-slice_fusion.5
  86.7 2.9 bitcast_dynamic-update-slice_fusion.5
  89.6 1.9 collective-permute-start.1
  92.6 4.1 collective-permute-done.1
  97.4 12.0 %collective-permute-start.1 = (f32[512,32]{0,1:T(8,128)S(1)}, f32[512,32]{0,1:T(8,128)S(1)}, u32[]{:S(2)}, u32[]{:S(2)}) collective-permute-start(f32[512,32]{0,1:T(8,128)S(1)} %get-tuple-element.651), channel_id=1, source_target_pairs={{0,4},{4,8},{8,12},{12,16},{16,20},{20,24},{24,28},{1,5},{5,9},{9,... | collective-permute-start | bytes 196616 | tf_op jit(solution)/shard_map/while/body/eval_jaxpr/ppermute | solution.py:23
  112.0 4.3 %collective-permute-start.1 = (f32[512,32]{0,1:T(8,128)S(1)}, f32[512,32]{0,1:T(8,128)S(1)}, u32[]{:S(2)}, u32[]{:S(2)}) collective-permute-start(f32[512,32]{0,1:T(8,128)S(1)} %get-tuple-element.651), channel_id=1, source_target_pairs={{0,4},{4,8},{8,12},{12,16},{16,20},{20,24},{24,28},{1,5},{5,9},{9,... | collective-permute-start | bytes 196616 | tf_op jit(solution)/shard_map/while/body/eval_jaxpr/ppermute | solution.py:23
  116.4 2.7 collective-permute-done.1
  119.8 12.9 %collective-permute-start.1 = (f32[512,32]{0,1:T(8,128)S(1)}, f32[512,32]{0,1:T(8,128)S(1)}, u32[]{:S(2)}, u32[]{:S(2)}) collective-permute-start(f32[512,32]{0,1:T(8,128)S(1)} %get-tuple-element.651), channel_id=1, source_target_pairs={{0,4},{4,8},{8,12},{12,16},{16,20},{20,24},{24,28},{1,5},{5,9},{9,... | collective-permute-start | bytes 196616 | tf_op jit(solution)/shard_map/while/body/eval_jaxpr/ppermute | solution.py:23
  135.3 5.2 %collective-permute-start.1 = (f32[512,32]{0,1:T(8,128)S(1)}, f32[512,32]{0,1:T(8,128)S(1)}, u32[]{:S(2)}, u32[]{:S(2)}) collective-permute-start(f32[512,32]{0,1:T(8,128)S(1)} %get-tuple-element.651), channel_id=1, source_target_pairs={{0,4},{4,8},{8,12},{12,16},{16,20},{20,24},{24,28},{1,5},{5,9},{9,... | collective-permute-start | bytes 196616 | tf_op jit(solution)/shard_map/while/body/eval_jaxpr/ppermute | solution.py:23
  143.1 12.0 %collective-permute-start.1 = (f32[512,32]{0,1:T(8,128)S(1)}, f32[512,32]{0,1:T(8,128)S(1)}, u32[]{:S(2)}, u32[]{:S(2)}) collective-permute-start(f32[512,32]{0,1:T(8,128)S(1)} %get-tuple-element.651), channel_id=1, source_target_pairs={{0,4},{4,8},{8,12},{12,16},{16,20},{20,24},{24,28},{1,5},{5,9},{9,... | collective-permute-start | bytes 196616 | tf_op jit(solution)/shard_map/while/body/eval_jaxpr/ppermute | solution.py:23
  157.0 155.7 %while.61 = (s32[]{:T(128)}, f32[4,512,32]{1,2,0:T(8,128)S(1)}, f32[512,32]{0,1:T(8,128)S(1)}, s32[]{:T(128)}, f32[4,512,32]{1,2,0:T(8,128)S(1)}, /*index=5*/f32[4,512,512]{2,1,0:T(8,128)}, s32[]{:T(128)}, s32[]{:T(128)}) while((s32[]{:T(128)}, f32[4,512,32]{1,2,0:T(8,128)S(1)}, f32[512,32]{0,1:T(8,128)S(1)}, s32[]{:T(128)}, ...), condition=%wide.region_14.15_spmd.clone, body=%wide.region_9.0_spmd.clone.sunk | while | flops 100810760 | bytes 2884979 | solution.py:79
  157.7 1.9 collective-permute-start
  159.8 5.4 %collective-permute-done = f32[512,32]{0,1:T(8,128)S(1)} collective-permute-done((f32[512,32]{0,1:T(8,128)S(1)}, f32[512,32]{0,1:T(8,128)S(1)}, u32[]{:S(2)}, u32[]{:S(2)}) %collective-permute-start) | collective-permute-done | bytes 65568 | tf_op jit(solution)/shard_map/while/body/eval_jaxpr/ppermute | solution.py:23
  165.9 2.2 collective-permute-start
  168.2 13.4 %collective-permute-done = f32[512,32]{0,1:T(8,128)S(1)} collective-permute-done((f32[512,32]{0,1:T(8,128)S(1)}, f32[512,32]{0,1:T(8,128)S(1)}, u32[]{:S(2)}, u32[]{:S(2)}) %collective-permute-start) | collective-permute-done | bytes 65568 | tf_op jit(solution)/shard_map/while/body/eval_jaxpr/ppermute | solution.py:23
  182.4 1.9 collective-permute-start
  184.4 5.0 %collective-permute-done = f32[512,32]{0,1:T(8,128)S(1)} collective-permute-done((f32[512,32]{0,1:T(8,128)S(1)}, f32[512,32]{0,1:T(8,128)S(1)}, u32[]{:S(2)}, u32[]{:S(2)}) %collective-permute-start) | collective-permute-done | bytes 65568 | tf_op jit(solution)/shard_map/while/body/eval_jaxpr/ppermute | solution.py:23
  190.1 1.9 collective-permute-start
  192.2 11.9 %collective-permute-done = f32[512,32]{0,1:T(8,128)S(1)} collective-permute-done((f32[512,32]{0,1:T(8,128)S(1)}, f32[512,32]{0,1:T(8,128)S(1)}, u32[]{:S(2)}, u32[]{:S(2)}) %collective-permute-start) | collective-permute-done | bytes 65568 | tf_op jit(solution)/shard_map/while/body/eval_jaxpr/ppermute | solution.py:23
  204.8 1.9 collective-permute-start
  206.9 62.3 %collective-permute-done = f32[512,32]{0,1:T(8,128)S(1)} collective-permute-done((f32[512,32]{0,1:T(8,128)S(1)}, f32[512,32]{0,1:T(8,128)S(1)}, u32[]{:S(2)}, u32[]{:S(2)}) %collective-permute-start) | collective-permute-done | bytes 65568 | tf_op jit(solution)/shard_map/while/body/eval_jaxpr/ppermute | solution.py:23
  269.2 12.4 %conditional.7 = (f32[512,32]{0,1:T(8,128)S(1)}, f32[4,512,32]{1,2,0:T(8,128)}) conditional(s32[]{:T(128)} %convert_element_type.27, () %tuple.153, (f32[4,512,32]{1,2,0:T(8,128)S(1)}, f32[4,512,512]{2,1,0:T(8,128)}, f32[512,32]{0,1:T(8,128)S(1)}) %tuple.154), branch_computations={%region_10.10_spmd, %region_11.13_spmd} | conditional | flops 100679680 | bytes 1836205 | solution.py:74
  270.0 11.7 %while.59 = (s32[]{:T(128)}, f32[512,32]{0,1:T(8,128)S(1)}, f32[4,512,32]{1,2,0:T(8,128)}, f32[4,512,32]{1,2,0:T(8,128)S(1)}, f32[4,512,512]{2,1,0:T(8,128)}, /*index=5*/s32[]{:T(128)}, s32[]{:T(128)}) while((s32[]{:T(128)}, f32[512,32]{0,1:T(8,128)S(1)}, f32[4,512,32]{1,2,0:T(8,128)}, f32[4,512,32]{1,2,0:T(8,128)S(1)}, ...), condition=%wide.region_13.12_spmd, body=%wide.region_12.11_spmd.sunk | while | flops 100679680 | bytes 1442905 | solution.py:53
  270.0 2.9 bitcast_dynamic-update-slice_fusion.4
  272.9 2.9 bitcast_dynamic-update-slice_fusion.4
  275.8 2.9 bitcast_dynamic-update-slice_fusion.4
  278.7 2.9 bitcast_dynamic-update-slice_fusion.4
  281.7 1.9 collective-permute-start
  284.6 3.2 collective-permute-done
  288.5 14.5 %collective-permute-start = (f32[512,32]{0,1:T(8,128)S(1)}, f32[512,32]{0,1:T(8,128)S(1)}, u32[]{:S(2)}, u32[]{:S(2)}) collective-permute-start(f32[512,32]{0,1:T(8,128)S(1)} %get-tuple-element.659), channel_id=1, source_target_pairs={{4,0},{8,4},{12,8},{16,12},{20,16},{24,20},{28,24},{5,1},{9,5},{13... | collective-permute-start | bytes 196616 | tf_op jit(solution)/shard_map/while/body/eval_jaxpr/ppermute | solution.py:23
  305.7 5.2 %collective-permute-start = (f32[512,32]{0,1:T(8,128)S(1)}, f32[512,32]{0,1:T(8,128)S(1)}, u32[]{:S(2)}, u32[]{:S(2)}) collective-permute-start(f32[512,32]{0,1:T(8,128)S(1)} %get-tuple-element.659), channel_id=1, source_target_pairs={{4,0},{8,4},{12,8},{16,12},{20,16},{24,20},{28,24},{5,1},{9,5},{13... | collective-permute-start | bytes 196616 | tf_op jit(solution)/shard_map/while/body/eval_jaxpr/ppermute | solution.py:23
  314.5 5.1 %all-to-all-start.1 = ((f32[4,1,16384]{2,1,0:T(1,128)}), f32[4,1,16384]{2,1,0:T(1,128)S(1)}, u32[]{:S(2)}, u32[]{:S(2)}) async-start(f32[4,1,16384]{2,1,0:T(1,128)} %reshape.6), calls=%async_computation.1 | async-start | bytes 524288 | tf_op jit(solution)/shard_map/all_to_all | solution.py:103
  319.6 4.3 %all-to-all-done.1 = f32[4,1,16384]{2,1,0:T(1,128)S(1)} async-done(((f32[4,1,16384]{2,1,0:T(1,128)}), f32[4,1,16384]{2,1,0:T(1,128)S(1)}, u32[]{:S(2)}, u32[]{:S(2)}) %all-to-all-start.1) | async-done | bytes 262176 | tf_op jit(solution)/shard_map/all_to_all | solution.py:103
  326.8 12.7 %collective-permute-start.2 = (f32[1,128,128]{1,2,0:T(8,128)S(1)}, f32[1,128,128]{1,2,0:T(8,128)S(1)}, u32[]{:S(2)}, u32[]{:S(2)}) collective-permute-start(f32[1,128,128]{1,2,0:T(8,128)S(1)} %bitcast.60), channel_id=1, source_target_pairs={{4,0},{8,4},{12,8},{16,12},{20,16},{24,20},{28,24},{5,1},{9,5},{13... | collective-permute-start | bytes 196616 | tf_op jit(solution)/shard_map/ppermute | solution.py:15
  339.5 1.9 collective-permute-start.3
  341.8 4.7 %collective-permute-done.3 = f32[1,128,128]{1,2,0:T(8,128)S(1)} collective-permute-done((f32[1,128,128]{1,2,0:T(8,128)S(1)}, f32[1,128,128]{1,2,0:T(8,128)S(1)}, u32[]{:S(2)}, u32[]{:S(2)}) %collective-permute-start.3) | collective-permute-done | bytes 65568 | tf_op jit(solution)/shard_map/ppermute | solution.py:14
  346.8 1.9 collective-permute-start.4
  348.7 2.4 collective-permute-start.5
  351.2 2.8 collective-permute-done.4
  354.0 3.8 collective-permute-done.5
  358.1 3.4 collective-permute-start.10
  361.5 2.5 collective-permute-start.11
  364.1 1.9 collective-permute-start.8
  366.1 2.4 collective-permute-start.9
  368.8 3.1 collective-permute-start.12
  371.9 1.9 collective-permute-start.13
  375.2 2.0 collective-permute-done.12
  377.2 3.8 collective-permute-done.13
  383.5 6.5 %all-reduce.7 = (f32[]{:T(128)}, f32[]{:T(128)}, f32[]{:T(128)}, f32[]{:T(128)}, f32[]{:T(128)}, /*index=5*/f32[]{:T(128)}, f32[]{:T(128)}, f32[]{:T(128)}) all-reduce(f32[]{:T(128)} %get-tuple-element.434, f32[]{:T(128)} %multiply_reduce_fusion.8, f32[]{:T(128)} %get-tuple-element.433, ...), channel_id=1, replica_groups=mesh['layer'=8,'split'=4] {'split'}, use_global_device_ids=true, to_apply=%region_19.20 | all-reduce | flops 8 | bytes 64 | tf_op jit(solution)/shard_map/psum | solution.py:107
  390.0 17.5 %all-reduce.6 = (f32[]{:T(128)}, f32[]{:T(128)}, f32[]{:T(128)}, f32[]{:T(128)}, f32[]{:T(128)}, /*index=5*/f32[]{:T(128)}, f32[]{:T(128)}, f32[]{:T(128)}) all-reduce(f32[]{:T(128)} %get-tuple-element.488, f32[]{:T(128)} %get-tuple-element.489, f32[]{:T(128)} %get-tuple-element.490, ...), channel_id=1, replica_groups=mesh['layer'=8,'split'=4] {'layer'}, use_global_device_ids=true, to_apply=%region_20.21 | all-reduce | flops 8 | bytes 64 | tf_op jit(solution)/shard_map/psum | solution.py:106
  (121 shorter events, 50.3 us)
Async XLA Ops:
  7.2 37.6 %all-gather.2.cloned.1.call-start = ((), (), s32[]{:S(2)}) async-start(), calls=%async_computation.2 | async-start | bytes 5242880 | tf_op jit(solution)/shard_map/all_gather | solution.py:86
  9.7 13.6 %all-to-all-start = ((f32[4,128,128]{1,0,2:T(4,128)}), f32[4,128,128]{1,0,2:T(4,128)S(1)}, u32[]{:S(2)}, u32[]{:S(2)}) async-start(f32[4,128,128]{1,0,2:T(4,128)} %copy.44), calls=%async_computation | async-start | bytes 524288 | tf_op jit(solution)/shard_map/all_to_all | solution.py:87
  14.7 326.8 %collective-permute-start.6 = (f32[1,128,128]{1,2,0:T(8,128)S(1)}, f32[1,128,128]{1,2,0:T(8,128)S(1)}, u32[]{:S(2)}, u32[]{:S(2)}) collective-permute-start(f32[1,128,128]{1,2,0:T(8,128)S(1)} %get-tuple-element.515), channel_id=1, source_target_pairs={{4,0},{8,4},{12,8},{16,12},{20,16},{24,20},{28,24},{5,1},{9,5},{13... | collective-permute-start | bytes 196616 | tf_op jit(solution)/shard_map/ppermute | solution.py:15
  18.0 323.5 %collective-permute-start.7 = (f32[1,128,128]{1,2,0:T(8,128)S(1)}, f32[1,128,128]{1,2,0:T(8,128)S(1)}, u32[]{:S(2)}, u32[]{:S(2)}) collective-permute-start(f32[1,128,128]{1,2,0:T(8,128)S(1)} %get-tuple-element.514), channel_id=1, source_target_pairs={{0,4},{4,8},{8,12},{12,16},{16,20},{20,24},{24,28},{1,5},{5,9},{9,... | collective-permute-start | bytes 196616 | tf_op jit(solution)/shard_map/ppermute | solution.py:14
  45.5 7.0 %collective-permute-start.1 = (f32[512,32]{0,1:T(8,128)S(1)}, f32[512,32]{0,1:T(8,128)S(1)}, u32[]{:S(2)}, u32[]{:S(2)}) collective-permute-start(f32[512,32]{0,1:T(8,128)S(1)} %get-tuple-element.651), channel_id=1, source_target_pairs={{0,4},{4,8},{8,12},{12,16},{16,20},{20,24},{24,28},{1,5},{5,9},{9,... | collective-permute-start | bytes 196616 | tf_op jit(solution)/shard_map/while/body/eval_jaxpr/ppermute | solution.py:23
  53.3 24.6 %collective-permute-start.1 = (f32[512,32]{0,1:T(8,128)S(1)}, f32[512,32]{0,1:T(8,128)S(1)}, u32[]{:S(2)}, u32[]{:S(2)}) collective-permute-start(f32[512,32]{0,1:T(8,128)S(1)} %get-tuple-element.651), channel_id=1, source_target_pairs={{0,4},{4,8},{8,12},{12,16},{16,20},{20,24},{24,28},{1,5},{5,9},{9,... | collective-permute-start | bytes 196616 | tf_op jit(solution)/shard_map/while/body/eval_jaxpr/ppermute | solution.py:23
  89.6 7.1 %collective-permute-start.1 = (f32[512,32]{0,1:T(8,128)S(1)}, f32[512,32]{0,1:T(8,128)S(1)}, u32[]{:S(2)}, u32[]{:S(2)}) collective-permute-start(f32[512,32]{0,1:T(8,128)S(1)} %get-tuple-element.651), channel_id=1, source_target_pairs={{0,4},{4,8},{8,12},{12,16},{16,20},{20,24},{24,28},{1,5},{5,9},{9,... | collective-permute-start | bytes 196616 | tf_op jit(solution)/shard_map/while/body/eval_jaxpr/ppermute | solution.py:23
  97.4 13.9 %collective-permute-start.1 = (f32[512,32]{0,1:T(8,128)S(1)}, f32[512,32]{0,1:T(8,128)S(1)}, u32[]{:S(2)}, u32[]{:S(2)}) collective-permute-start(f32[512,32]{0,1:T(8,128)S(1)} %get-tuple-element.651), channel_id=1, source_target_pairs={{0,4},{4,8},{8,12},{12,16},{16,20},{20,24},{24,28},{1,5},{5,9},{9,... | collective-permute-start | bytes 196616 | tf_op jit(solution)/shard_map/while/body/eval_jaxpr/ppermute | solution.py:23
  112.0 7.0 %collective-permute-start.1 = (f32[512,32]{0,1:T(8,128)S(1)}, f32[512,32]{0,1:T(8,128)S(1)}, u32[]{:S(2)}, u32[]{:S(2)}) collective-permute-start(f32[512,32]{0,1:T(8,128)S(1)} %get-tuple-element.651), channel_id=1, source_target_pairs={{0,4},{4,8},{8,12},{12,16},{16,20},{20,24},{24,28},{1,5},{5,9},{9,... | collective-permute-start | bytes 196616 | tf_op jit(solution)/shard_map/while/body/eval_jaxpr/ppermute | solution.py:23
  119.8 14.8 %collective-permute-start.1 = (f32[512,32]{0,1:T(8,128)S(1)}, f32[512,32]{0,1:T(8,128)S(1)}, u32[]{:S(2)}, u32[]{:S(2)}) collective-permute-start(f32[512,32]{0,1:T(8,128)S(1)} %get-tuple-element.651), channel_id=1, source_target_pairs={{0,4},{4,8},{8,12},{12,16},{16,20},{20,24},{24,28},{1,5},{5,9},{9,... | collective-permute-start | bytes 196616 | tf_op jit(solution)/shard_map/while/body/eval_jaxpr/ppermute | solution.py:23
  135.3 7.0 %collective-permute-start.1 = (f32[512,32]{0,1:T(8,128)S(1)}, f32[512,32]{0,1:T(8,128)S(1)}, u32[]{:S(2)}, u32[]{:S(2)}) collective-permute-start(f32[512,32]{0,1:T(8,128)S(1)} %get-tuple-element.651), channel_id=1, source_target_pairs={{0,4},{4,8},{8,12},{12,16},{16,20},{20,24},{24,28},{1,5},{5,9},{9,... | collective-permute-start | bytes 196616 | tf_op jit(solution)/shard_map/while/body/eval_jaxpr/ppermute | solution.py:23
  143.1 13.9 %collective-permute-start.1 = (f32[512,32]{0,1:T(8,128)S(1)}, f32[512,32]{0,1:T(8,128)S(1)}, u32[]{:S(2)}, u32[]{:S(2)}) collective-permute-start(f32[512,32]{0,1:T(8,128)S(1)} %get-tuple-element.651), channel_id=1, source_target_pairs={{0,4},{4,8},{8,12},{12,16},{16,20},{20,24},{24,28},{1,5},{5,9},{9,... | collective-permute-start | bytes 196616 | tf_op jit(solution)/shard_map/while/body/eval_jaxpr/ppermute | solution.py:23
  157.7 7.4 %collective-permute-start = (f32[512,32]{0,1:T(8,128)S(1)}, f32[512,32]{0,1:T(8,128)S(1)}, u32[]{:S(2)}, u32[]{:S(2)}) collective-permute-start(f32[512,32]{0,1:T(8,128)S(1)} %get-tuple-element.659), channel_id=1, source_target_pairs={{4,0},{8,4},{12,8},{16,12},{20,16},{24,20},{28,24},{5,1},{9,5},{13... | collective-permute-start | bytes 196616 | tf_op jit(solution)/shard_map/while/body/eval_jaxpr/ppermute | solution.py:23
  165.9 15.7 %collective-permute-start = (f32[512,32]{0,1:T(8,128)S(1)}, f32[512,32]{0,1:T(8,128)S(1)}, u32[]{:S(2)}, u32[]{:S(2)}) collective-permute-start(f32[512,32]{0,1:T(8,128)S(1)} %get-tuple-element.659), channel_id=1, source_target_pairs={{4,0},{8,4},{12,8},{16,12},{20,16},{24,20},{28,24},{5,1},{9,5},{13... | collective-permute-start | bytes 196616 | tf_op jit(solution)/shard_map/while/body/eval_jaxpr/ppermute | solution.py:23
  182.4 7.0 %collective-permute-start = (f32[512,32]{0,1:T(8,128)S(1)}, f32[512,32]{0,1:T(8,128)S(1)}, u32[]{:S(2)}, u32[]{:S(2)}) collective-permute-start(f32[512,32]{0,1:T(8,128)S(1)} %get-tuple-element.659), channel_id=1, source_target_pairs={{4,0},{8,4},{12,8},{16,12},{20,16},{24,20},{28,24},{5,1},{9,5},{13... | collective-permute-start | bytes 196616 | tf_op jit(solution)/shard_map/while/body/eval_jaxpr/ppermute | solution.py:23
  190.1 14.0 %collective-permute-start = (f32[512,32]{0,1:T(8,128)S(1)}, f32[512,32]{0,1:T(8,128)S(1)}, u32[]{:S(2)}, u32[]{:S(2)}) collective-permute-start(f32[512,32]{0,1:T(8,128)S(1)} %get-tuple-element.659), channel_id=1, source_target_pairs={{4,0},{8,4},{12,8},{16,12},{20,16},{24,20},{28,24},{5,1},{9,5},{13... | collective-permute-start | bytes 196616 | tf_op jit(solution)/shard_map/while/body/eval_jaxpr/ppermute | solution.py:23
  204.8 64.4 %collective-permute-start = (f32[512,32]{0,1:T(8,128)S(1)}, f32[512,32]{0,1:T(8,128)S(1)}, u32[]{:S(2)}, u32[]{:S(2)}) collective-permute-start(f32[512,32]{0,1:T(8,128)S(1)} %get-tuple-element.659), channel_id=1, source_target_pairs={{4,0},{8,4},{12,8},{16,12},{20,16},{24,20},{28,24},{5,1},{9,5},{13... | collective-permute-start | bytes 196616 | tf_op jit(solution)/shard_map/while/body/eval_jaxpr/ppermute | solution.py:23
  281.7 6.2 %collective-permute-start = (f32[512,32]{0,1:T(8,128)S(1)}, f32[512,32]{0,1:T(8,128)S(1)}, u32[]{:S(2)}, u32[]{:S(2)}) collective-permute-start(f32[512,32]{0,1:T(8,128)S(1)} %get-tuple-element.659), channel_id=1, source_target_pairs={{4,0},{8,4},{12,8},{16,12},{20,16},{24,20},{28,24},{5,1},{9,5},{13... | collective-permute-start | bytes 196616 | tf_op jit(solution)/shard_map/while/body/eval_jaxpr/ppermute | solution.py:23
  288.5 16.4 %collective-permute-start = (f32[512,32]{0,1:T(8,128)S(1)}, f32[512,32]{0,1:T(8,128)S(1)}, u32[]{:S(2)}, u32[]{:S(2)}) collective-permute-start(f32[512,32]{0,1:T(8,128)S(1)} %get-tuple-element.659), channel_id=1, source_target_pairs={{4,0},{8,4},{12,8},{16,12},{20,16},{24,20},{28,24},{5,1},{9,5},{13... | collective-permute-start | bytes 196616 | tf_op jit(solution)/shard_map/while/body/eval_jaxpr/ppermute | solution.py:23
  305.7 7.0 %collective-permute-start = (f32[512,32]{0,1:T(8,128)S(1)}, f32[512,32]{0,1:T(8,128)S(1)}, u32[]{:S(2)}, u32[]{:S(2)}) collective-permute-start(f32[512,32]{0,1:T(8,128)S(1)} %get-tuple-element.659), channel_id=1, source_target_pairs={{4,0},{8,4},{12,8},{16,12},{20,16},{24,20},{28,24},{5,1},{9,5},{13... | collective-permute-start | bytes 196616 | tf_op jit(solution)/shard_map/while/body/eval_jaxpr/ppermute | solution.py:23
  314.5 9.4 %all-to-all-start.1 = ((f32[4,1,16384]{2,1,0:T(1,128)}), f32[4,1,16384]{2,1,0:T(1,128)S(1)}, u32[]{:S(2)}, u32[]{:S(2)}) async-start(f32[4,1,16384]{2,1,0:T(1,128)} %reshape.6), calls=%async_computation.1 | async-start | bytes 524288 | tf_op jit(solution)/shard_map/all_to_all | solution.py:103
  326.8 15.1 %collective-permute-start.2 = (f32[1,128,128]{1,2,0:T(8,128)S(1)}, f32[1,128,128]{1,2,0:T(8,128)S(1)}, u32[]{:S(2)}, u32[]{:S(2)}) collective-permute-start(f32[1,128,128]{1,2,0:T(8,128)S(1)} %bitcast.60), channel_id=1, source_target_pairs={{4,0},{8,4},{12,8},{16,12},{20,16},{24,20},{28,24},{5,1},{9,5},{13... | collective-permute-start | bytes 196616 | tf_op jit(solution)/shard_map/ppermute | solution.py:15
  339.5 7.1 %collective-permute-start.3 = (f32[1,128,128]{1,2,0:T(8,128)S(1)}, f32[1,128,128]{1,2,0:T(8,128)S(1)}, u32[]{:S(2)}, u32[]{:S(2)}) collective-permute-start(f32[1,128,128]{1,2,0:T(8,128)S(1)} %bitcast.61), channel_id=1, source_target_pairs={{0,4},{4,8},{8,12},{12,16},{16,20},{20,24},{24,28},{1,5},{5,9},{9,... | collective-permute-start | bytes 196616 | tf_op jit(solution)/shard_map/ppermute | solution.py:14
  346.8 7.2 %collective-permute-start.4 = (f32[6,1,128]{1,2,0:T(8,128)S(1)}, f32[6,1,128]{1,2,0:T(8,128)S(1)}, u32[]{:S(2)}, u32[]{:S(2)}) collective-permute-start(f32[6,1,128]{1,2,0:T(8,128)S(1)} %get-tuple-element.508), channel_id=1, source_target_pairs={{1,0},{2,1},{3,2},{5,4},{6,5},{7,6},{9,8},{10,9},{11,10},{13,12},{... | collective-permute-start | bytes 9224 | tf_op jit(solution)/shard_map/ppermute | solution.py:15
  348.7 9.1 %collective-permute-start.5 = (f32[6,1,128]{1,2,0:T(8,128)S(1)}, f32[6,1,128]{1,2,0:T(8,128)S(1)}, u32[]{:S(2)}, u32[]{:S(2)}) collective-permute-start(f32[6,1,128]{1,2,0:T(8,128)S(1)} %get-tuple-element.509), channel_id=1, source_target_pairs={{0,1},{1,2},{2,3},{4,5},{5,6},{6,7},{8,9},{9,10},{10,11},{12,13},{... | collective-permute-start | bytes 9224 | tf_op jit(solution)/shard_map/ppermute | solution.py:14
  358.1 10.4 %collective-permute-start.10 = (f32[1,128,128]{1,2,0:T(8,128)S(1)}, f32[1,128,128]{1,2,0:T(8,128)S(1)}, u32[]{:S(2)}, u32[]{:S(2)}) collective-permute-start(f32[1,128,128]{1,2,0:T(8,128)S(1)} %get-tuple-element.511), channel_id=1, source_target_pairs={{4,0},{8,4},{12,8},{16,12},{20,16},{24,20},{28,24},{5,1},{9,5},{13... | collective-permute-start | bytes 196616 | tf_op jit(solution)/shard_map/ppermute | solution.py:15
  361.5 7.1 %collective-permute-start.11 = (f32[1,128,128]{1,2,0:T(8,128)S(1)}, f32[1,128,128]{1,2,0:T(8,128)S(1)}, u32[]{:S(2)}, u32[]{:S(2)}) collective-permute-start(f32[1,128,128]{1,2,0:T(8,128)S(1)} %get-tuple-element.510), channel_id=1, source_target_pairs={{0,4},{4,8},{8,12},{12,16},{16,20},{20,24},{24,28},{1,5},{5,9},{9,... | collective-permute-start | bytes 196616 | tf_op jit(solution)/shard_map/ppermute | solution.py:14
  364.1 9.7 %collective-permute-start.8 = (f32[6,1,128]{1,2,0:T(8,128)S(1)}, f32[6,1,128]{1,2,0:T(8,128)S(1)}, u32[]{:S(2)}, u32[]{:S(2)}) collective-permute-start(f32[6,1,128]{1,2,0:T(8,128)S(1)} %get-tuple-element.506), channel_id=1, source_target_pairs={{1,0},{2,1},{3,2},{5,4},{6,5},{7,6},{9,8},{10,9},{11,10},{13,12},{... | collective-permute-start | bytes 9224 | tf_op jit(solution)/shard_map/ppermute | solution.py:15
  366.1 9.1 %collective-permute-start.9 = (f32[6,1,128]{1,2,0:T(8,128)S(1)}, f32[6,1,128]{1,2,0:T(8,128)S(1)}, u32[]{:S(2)}, u32[]{:S(2)}) collective-permute-start(f32[6,1,128]{1,2,0:T(8,128)S(1)} %get-tuple-element.507), channel_id=1, source_target_pairs={{0,1},{1,2},{2,3},{4,5},{5,6},{6,7},{8,9},{9,10},{10,11},{12,13},{... | collective-permute-start | bytes 9224 | tf_op jit(solution)/shard_map/ppermute | solution.py:14
  368.8 8.4 %collective-permute-start.12 = (f32[6,1,128]{1,2,0:T(8,128)S(1)}, f32[6,1,128]{1,2,0:T(8,128)S(1)}, u32[]{:S(2)}, u32[]{:S(2)}) collective-permute-start(f32[6,1,128]{1,2,0:T(8,128)S(1)} %get-tuple-element.504), channel_id=1, source_target_pairs={{1,0},{2,1},{3,2},{5,4},{6,5},{7,6},{9,8},{10,9},{11,10},{13,12},{... | collective-permute-start | bytes 9224 | tf_op jit(solution)/shard_map/ppermute | solution.py:15
  371.9 9.1 %collective-permute-start.13 = (f32[6,1,128]{1,2,0:T(8,128)S(1)}, f32[6,1,128]{1,2,0:T(8,128)S(1)}, u32[]{:S(2)}, u32[]{:S(2)}) collective-permute-start(f32[6,1,128]{1,2,0:T(8,128)S(1)} %get-tuple-element.505), channel_id=1, source_target_pairs={{0,1},{1,2},{2,3},{4,5},{5,6},{6,7},{8,9},{9,10},{10,11},{12,13},{... | collective-permute-start | bytes 9224 | tf_op jit(solution)/shard_map/ppermute | solution.py:14
Sparse Core Ops, SparseCore 0:
  9.5 35.1 all-gather.1
